TPU v7x, 32 devices: a whole 2x2x4 slice. The times are simulated.
32 devices in a mesh: elem: 16 (over z, y, core), test: 2 (over x).
Axes of the slice: x: 2, y: 2, z: 4, core: 2. Of those that a mesh axis runs over, the one named last changes fastest.
Arguments:
- mode_fields: bfloat16 [64, 3, 65536], P('test', None, 'elem'), may hold values from -6 to 6
- elem_type: int32 [128], P('elem'), may hold values from 0 to 3
- type_scales: float32 [4, 3], replicated, may hold values from 0.5 to 2
Outputs:
- conv_tensor: float32 [64, 64, 64], P('test', 'elem')
All inputs are finite; a program needn't handle non-finite values.
Results may differ from a plain program's by a relative error of at most 0.0051.
Values may be sent and summed in bfloat16 or wider, within the bound.
A program may use at most 64 MiB of HBM per device.

v0:
```python
import jax
import jax.numpy as jnp
import numpy as np
from jax import lax
from jax.sharding import PartitionSpec as P

Q = 8


block_modes = 4


def legendre_top(points, degree):
    before = points * 0.0 + 1.0
    current = points
    for order in range(2, degree + 1):
        following = ((2 * order - 1) * points * current - (order - 1) * before) / order
        before = current
        current = following
    return (current, before)


def lobatto_tables(order_points):
    degree = order_points - 1
    lobatto_nodes = np.cos(np.pi * np.arange(degree + 1) / degree)
    for sweep in range(100):
        top, lower = legendre_top(lobatto_nodes, degree)
        lobatto_nodes = lobatto_nodes - (lobatto_nodes * top - lower) / ((degree + 1) * top)
    lobatto_nodes = lobatto_nodes[::-1].copy()
    lobatto_nodes[0] = -1.0
    lobatto_nodes[-1] = 1.0
    values, unused = legendre_top(lobatto_nodes, degree)
    weights = 2.0 / (degree * (degree + 1) * values**2)
    identity = np.eye(order_points)
    distance = lobatto_nodes[:, None] - lobatto_nodes[None, :]
    spacing = np.where(identity > 0, 1.0, distance)
    derivative = np.where(identity > 0, 0.0, values[:, None] / values[None, :] / spacing)
    corner = degree * (degree + 1) / 4.0
    ends = np.concatenate([[-corner], np.zeros(degree - 1), [corner]])
    derivative = derivative + identity * ends[None, :]
    square_eye = np.eye(order_points * order_points)
    along_r = np.kron(square_eye, derivative)
    along_s = np.kron(identity, np.kron(derivative, identity))
    along_t = np.kron(derivative, square_eye)
    table = np.concatenate([along_r.T, along_s.T, along_t.T], axis=1)
    cube_weights = np.kron(weights, np.kron(weights, weights))
    return (table.astype(np.float32), cube_weights.astype(np.float32))


def element_scales(types, type_scales):
    picks = (types[:, None] == jnp.arange(type_scales.shape[0], dtype=jnp.int32)[None, :]).astype(
        jnp.float32
    )
    return jnp.sum(picks[:, :, None] * type_scales[None, :, :], axis=1)


def gradient(fields, scales, table, cube):
    mode_count = fields.shape[0]
    elements = fields.shape[2] // cube
    flat = fields.reshape(mode_count * 3 * elements, cube)
    derived = jnp.dot(flat, table, preferred_element_type=jnp.float32).reshape(
        mode_count, 3, elements, 3, cube
    )
    return (derived * scales[None, None, :, :, None]).astype(jnp.bfloat16)


def project(test_fields, trial_fields, grads, quadrature):
    test_modes = test_fields.shape[0]
    trial_modes = trial_fields.shape[0]
    grad_modes = grads.shape[0]
    blocks = grads.reshape((grad_modes // block_modes, block_modes) + grads.shape[1:])
    test_wide = test_fields.astype(jnp.float32)

    def one_block(grad_block):
        grad_wide = grad_block.astype(jnp.float32)
        summed = test_wide[:, None, 0, :, None, :] * grad_wide[None, :, 0]
        summed = summed + test_wide[:, None, 1, :, None, :] * grad_wide[None, :, 1]
        summed = summed + test_wide[:, None, 2, :, None, :] * grad_wide[None, :, 2]
        pairs = (summed * quadrature[None, None, :, None, :]).astype(jnp.bfloat16)
        return jnp.einsum(
            "ikedp,jdep->ijk", pairs, trial_fields, preferred_element_type=jnp.float32
        )

    result = lax.map(one_block, blocks)
    return result.transpose(1, 2, 0, 3).reshape(test_modes, trial_modes, grad_modes)


def body(mode_fields, elem_type, type_scales):
    table, cube_weights = lobatto_tables(Q)
    table = jnp.asarray(table).astype(jnp.bfloat16)
    point_weights = jnp.asarray(cube_weights).astype(jnp.float32)
    cube = Q**3
    total_points = mode_fields.shape[2] * lax.axis_size("elem")
    gathered = lax.all_gather(mode_fields, "test", axis=0, tiled=True)
    elements = mode_fields.shape[2] // cube
    scales = element_scales(elem_type, type_scales)
    quadrature = point_weights[None, :] / jnp.prod(scales, axis=1)[:, None]
    grads = gradient(gathered, scales, table, cube)
    partial_value = project(
        mode_fields.reshape(mode_fields.shape[0], 3, elements, cube),
        gathered.reshape(gathered.shape[0], 3, elements, cube),
        grads,
        quadrature,
    )
    summed = lax.psum_scatter(partial_value, "elem", scatter_dimension=1, tiled=True)
    return summed * float(total_points) ** (-0.5)


def solution(mesh):
    placed = (P("test", None, "elem"), P("elem"), P())
    return jax.shard_map(
        body, mesh=mesh, in_specs=placed, out_specs=P("test", "elem", None), check_vma=False
    )
```

profile of v0, /device:TPU:0, one launch (start us, length us, event | category | flops | bytes accessed | tf_op | source)
XLA Modules:
  0.0 182.2 jit_solution(7041535098381613878)
XLA Ops:
  7.3 1.3 convert_element_type.34
  9.7 29.2 %all-gather.2.cloned.1.call-done = bf16[64,3,4096]{2,0,1:T(8,128)(2,1)} async-done(((bf16[32,3,4096]{2,0,1:T(8,128)(2,1)}), bf16[64,3,4096]{2,0,1:T(8,128)(2,1)}) %all-gather.2.cloned.1.call-update) | async-done | bytes 1572880 | tf_op jit(solution)/shard_map/all_gather | solution.py:94
  38.8 1.6 copy.40
  40.4 6.7 %fusion.11 = bf16[64,3,8,3,512]{4,0,2,1,3:T(8,128)(2,1)} fusion(f32[8,3]{0,1:T(4,128)S(1)} %multiply_reduce_fusion, bf16[3,512,512,1,1]{2,1,4,3,0:T(8,128)(2,1)} %constant.28, bf16[3,8,8,8,512]{4,3,2,1,0:T(8,128)(2,1)} %bitcast.79), kind=kOutput, calls=%fused_computation.17 | convolution fusion | flops 2420637696 | bytes 7864416 | tf_op jit(solution)/shard_map/dot_general | solution.py:61
  47.2 7.7 %reshape.50 = bf16[16,4,3,8,3,512]{5,1,0,3,2,4:T(4,128)(2,1)} reshape(bf16[64,3,8,3,512]{4,0,2,1,3:T(8,128)(2,1)} %fusion.11) | data formatting | bytes 9437184 | tf_op jit(solution)/shard_map/reshape | solution.py:71
  54.9 58.1 %while.11 = (s32[]{:T(128)}, f32[16,32,64,4]{2,1,3,0:T(8,128)}, f32[32,3,8,512]{3,0,2,1:T(8,128)S(1)}, bf16[16,4,3,8,3,512]{5,1,0,3,2,4:T(4,128)(2,1)}, bf16[64,...) while((s32[]{:T(128)}, f32[16,32,64,4]{2,1,3,0:T(8,128)}, ...), condition=%wide.region_3.4_spmd.clone, body=%wide.region_2.3_spmd.clone.sunk | while | flops 212488192 | bytes 9636473 | solution.py:84
  56.3 2.1 %fusion.20 = f32[16,32,64,4]{2,1,3,0:T(8,128)} fusion(f32[16,32,64,4]{2,1,3,0:T(8,128)} %get-tuple-element.168, s32[]{:T(128)} %get-tuple-element.167, bf16[64,3,8,512]{3,0,2,1:T(8,128)(2,1)S(1)} %get-tuple-element.179, f32[8,512]{1,0:T(8,128)S(1)} %broadcast_divide_fusion.2, f32[4,8,3,512]{3,1,0,2:T(8,128)S(1)} %get-tuple-element.153, ...), kind=kOutput, calls=%fused_computation.5.clone.1 | convolution fusion | flops 212336640 | bytes 3817984 | tf_op jit(solution)/shard_map/while/body/eval_jaxpr/ikedp,jdep->ijk/dot_general | solution.py:80
  60.0 2.2 %fusion.20 = f32[16,32,64,4]{2,1,3,0:T(8,128)} fusion(f32[16,32,64,4]{2,1,3,0:T(8,128)} %get-tuple-element.168, s32[]{:T(128)} %get-tuple-element.167, bf16[64,3,8,512]{3,0,2,1:T(8,128)(2,1)S(1)} %get-tuple-element.179, f32[8,512]{1,0:T(8,128)S(1)} %broadcast_divide_fusion.2, f32[4,8,3,512]{3,1,0,2:T(8,128)S(1)} %get-tuple-element.153, ...), kind=kOutput, calls=%fused_computation.5.clone.1 | convolution fusion | flops 212336640 | bytes 3817984 | tf_op jit(solution)/shard_map/while/body/eval_jaxpr/ikedp,jdep->ijk/dot_general | solution.py:80
  63.6 2.2 %fusion.20 = f32[16,32,64,4]{2,1,3,0:T(8,128)} fusion(f32[16,32,64,4]{2,1,3,0:T(8,128)} %get-tuple-element.168, s32[]{:T(128)} %get-tuple-element.167, bf16[64,3,8,512]{3,0,2,1:T(8,128)(2,1)S(1)} %get-tuple-element.179, f32[8,512]{1,0:T(8,128)S(1)} %broadcast_divide_fusion.2, f32[4,8,3,512]{3,1,0,2:T(8,128)S(1)} %get-tuple-element.153, ...), kind=kOutput, calls=%fused_computation.5.clone.1 | convolution fusion | flops 212336640 | bytes 3817984 | tf_op jit(solution)/shard_map/while/body/eval_jaxpr/ikedp,jdep->ijk/dot_general | solution.py:80
  67.2 2.2 %fusion.20 = f32[16,32,64,4]{2,1,3,0:T(8,128)} fusion(f32[16,32,64,4]{2,1,3,0:T(8,128)} %get-tuple-element.168, s32[]{:T(128)} %get-tuple-element.167, bf16[64,3,8,512]{3,0,2,1:T(8,128)(2,1)S(1)} %get-tuple-element.179, f32[8,512]{1,0:T(8,128)S(1)} %broadcast_divide_fusion.2, f32[4,8,3,512]{3,1,0,2:T(8,128)S(1)} %get-tuple-element.153, ...), kind=kOutput, calls=%fused_computation.5.clone.1 | convolution fusion | flops 212336640 | bytes 3817984 | tf_op jit(solution)/shard_map/while/body/eval_jaxpr/ikedp,jdep->ijk/dot_general | solution.py:80
  70.9 2.1 %fusion.20 = f32[16,32,64,4]{2,1,3,0:T(8,128)} fusion(f32[16,32,64,4]{2,1,3,0:T(8,128)} %get-tuple-element.168, s32[]{:T(128)} %get-tuple-element.167, bf16[64,3,8,512]{3,0,2,1:T(8,128)(2,1)S(1)} %get-tuple-element.179, f32[8,512]{1,0:T(8,128)S(1)} %broadcast_divide_fusion.2, f32[4,8,3,512]{3,1,0,2:T(8,128)S(1)} %get-tuple-element.153, ...), kind=kOutput, calls=%fused_computation.5.clone.1 | convolution fusion | flops 212336640 | bytes 3817984 | tf_op jit(solution)/shard_map/while/body/eval_jaxpr/ikedp,jdep->ijk/dot_general | solution.py:80
  74.5 2.2 %fusion.20 = f32[16,32,64,4]{2,1,3,0:T(8,128)} fusion(f32[16,32,64,4]{2,1,3,0:T(8,128)} %get-tuple-element.168, s32[]{:T(128)} %get-tuple-element.167, bf16[64,3,8,512]{3,0,2,1:T(8,128)(2,1)S(1)} %get-tuple-element.179, f32[8,512]{1,0:T(8,128)S(1)} %broadcast_divide_fusion.2, f32[4,8,3,512]{3,1,0,2:T(8,128)S(1)} %get-tuple-element.153, ...), kind=kOutput, calls=%fused_computation.5.clone.1 | convolution fusion | flops 212336640 | bytes 3817984 | tf_op jit(solution)/shard_map/while/body/eval_jaxpr/ikedp,jdep->ijk/dot_general | solution.py:80
  78.1 2.2 %fusion.20 = f32[16,32,64,4]{2,1,3,0:T(8,128)} fusion(f32[16,32,64,4]{2,1,3,0:T(8,128)} %get-tuple-element.168, s32[]{:T(128)} %get-tuple-element.167, bf16[64,3,8,512]{3,0,2,1:T(8,128)(2,1)S(1)} %get-tuple-element.179, f32[8,512]{1,0:T(8,128)S(1)} %broadcast_divide_fusion.2, f32[4,8,3,512]{3,1,0,2:T(8,128)S(1)} %get-tuple-element.153, ...), kind=kOutput, calls=%fused_computation.5.clone.1 | convolution fusion | flops 212336640 | bytes 3817984 | tf_op jit(solution)/shard_map/while/body/eval_jaxpr/ikedp,jdep->ijk/dot_general | solution.py:80
  81.8 2.1 %fusion.20 = f32[16,32,64,4]{2,1,3,0:T(8,128)} fusion(f32[16,32,64,4]{2,1,3,0:T(8,128)} %get-tuple-element.168, s32[]{:T(128)} %get-tuple-element.167, bf16[64,3,8,512]{3,0,2,1:T(8,128)(2,1)S(1)} %get-tuple-element.179, f32[8,512]{1,0:T(8,128)S(1)} %broadcast_divide_fusion.2, f32[4,8,3,512]{3,1,0,2:T(8,128)S(1)} %get-tuple-element.153, ...), kind=kOutput, calls=%fused_computation.5.clone.1 | convolution fusion | flops 212336640 | bytes 3817984 | tf_op jit(solution)/shard_map/while/body/eval_jaxpr/ikedp,jdep->ijk/dot_general | solution.py:80
  85.4 2.2 %fusion.20 = f32[16,32,64,4]{2,1,3,0:T(8,128)} fusion(f32[16,32,64,4]{2,1,3,0:T(8,128)} %get-tuple-element.168, s32[]{:T(128)} %get-tuple-element.167, bf16[64,3,8,512]{3,0,2,1:T(8,128)(2,1)S(1)} %get-tuple-element.179, f32[8,512]{1,0:T(8,128)S(1)} %broadcast_divide_fusion.2, f32[4,8,3,512]{3,1,0,2:T(8,128)S(1)} %get-tuple-element.153, ...), kind=kOutput, calls=%fused_computation.5.clone.1 | convolution fusion | flops 212336640 | bytes 3817984 | tf_op jit(solution)/shard_map/while/body/eval_jaxpr/ikedp,jdep->ijk/dot_general | solution.py:80
  89.0 2.2 %fusion.20 = f32[16,32,64,4]{2,1,3,0:T(8,128)} fusion(f32[16,32,64,4]{2,1,3,0:T(8,128)} %get-tuple-element.168, s32[]{:T(128)} %get-tuple-element.167, bf16[64,3,8,512]{3,0,2,1:T(8,128)(2,1)S(1)} %get-tuple-element.179, f32[8,512]{1,0:T(8,128)S(1)} %broadcast_divide_fusion.2, f32[4,8,3,512]{3,1,0,2:T(8,128)S(1)} %get-tuple-element.153, ...), kind=kOutput, calls=%fused_computation.5.clone.1 | convolution fusion | flops 212336640 | bytes 3817984 | tf_op jit(solution)/shard_map/while/body/eval_jaxpr/ikedp,jdep->ijk/dot_general | solution.py:80
  92.6 2.2 %fusion.20 = f32[16,32,64,4]{2,1,3,0:T(8,128)} fusion(f32[16,32,64,4]{2,1,3,0:T(8,128)} %get-tuple-element.168, s32[]{:T(128)} %get-tuple-element.167, bf16[64,3,8,512]{3,0,2,1:T(8,128)(2,1)S(1)} %get-tuple-element.179, f32[8,512]{1,0:T(8,128)S(1)} %broadcast_divide_fusion.2, f32[4,8,3,512]{3,1,0,2:T(8,128)S(1)} %get-tuple-element.153, ...), kind=kOutput, calls=%fused_computation.5.clone.1 | convolution fusion | flops 212336640 | bytes 3817984 | tf_op jit(solution)/shard_map/while/body/eval_jaxpr/ikedp,jdep->ijk/dot_general | solution.py:80
  96.3 2.2 %fusion.20 = f32[16,32,64,4]{2,1,3,0:T(8,128)} fusion(f32[16,32,64,4]{2,1,3,0:T(8,128)} %get-tuple-element.168, s32[]{:T(128)} %get-tuple-element.167, bf16[64,3,8,512]{3,0,2,1:T(8,128)(2,1)S(1)} %get-tuple-element.179, f32[8,512]{1,0:T(8,128)S(1)} %broadcast_divide_fusion.2, f32[4,8,3,512]{3,1,0,2:T(8,128)S(1)} %get-tuple-element.153, ...), kind=kOutput, calls=%fused_computation.5.clone.1 | convolution fusion | flops 212336640 | bytes 3817984 | tf_op jit(solution)/shard_map/while/body/eval_jaxpr/ikedp,jdep->ijk/dot_general | solution.py:80
  99.9 2.2 %fusion.20 = f32[16,32,64,4]{2,1,3,0:T(8,128)} fusion(f32[16,32,64,4]{2,1,3,0:T(8,128)} %get-tuple-element.168, s32[]{:T(128)} %get-tuple-element.167, bf16[64,3,8,512]{3,0,2,1:T(8,128)(2,1)S(1)} %get-tuple-element.179, f32[8,512]{1,0:T(8,128)S(1)} %broadcast_divide_fusion.2, f32[4,8,3,512]{3,1,0,2:T(8,128)S(1)} %get-tuple-element.153, ...), kind=kOutput, calls=%fused_computation.5.clone.1 | convolution fusion | flops 212336640 | bytes 3817984 | tf_op jit(solution)/shard_map/while/body/eval_jaxpr/ikedp,jdep->ijk/dot_general | solution.py:80
  103.5 2.2 %fusion.20 = f32[16,32,64,4]{2,1,3,0:T(8,128)} fusion(f32[16,32,64,4]{2,1,3,0:T(8,128)} %get-tuple-element.168, s32[]{:T(128)} %get-tuple-element.167, bf16[64,3,8,512]{3,0,2,1:T(8,128)(2,1)S(1)} %get-tuple-element.179, f32[8,512]{1,0:T(8,128)S(1)} %broadcast_divide_fusion.2, f32[4,8,3,512]{3,1,0,2:T(8,128)S(1)} %get-tuple-element.153, ...), kind=kOutput, calls=%fused_computation.5.clone.1 | convolution fusion | flops 212336640 | bytes 3817984 | tf_op jit(solution)/shard_map/while/body/eval_jaxpr/ikedp,jdep->ijk/dot_general | solution.py:80
  107.2 2.2 %fusion.20 = f32[16,32,64,4]{2,1,3,0:T(8,128)} fusion(f32[16,32,64,4]{2,1,3,0:T(8,128)} %get-tuple-element.168, s32[]{:T(128)} %get-tuple-element.167, bf16[64,3,8,512]{3,0,2,1:T(8,128)(2,1)S(1)} %get-tuple-element.179, f32[8,512]{1,0:T(8,128)S(1)} %broadcast_divide_fusion.2, f32[4,8,3,512]{3,1,0,2:T(8,128)S(1)} %get-tuple-element.153, ...), kind=kOutput, calls=%fused_computation.5.clone.1 | convolution fusion | flops 212336640 | bytes 3817984 | tf_op jit(solution)/shard_map/while/body/eval_jaxpr/ikedp,jdep->ijk/dot_general | solution.py:80
  110.8 2.1 %fusion.20 = f32[16,32,64,4]{2,1,3,0:T(8,128)} fusion(f32[16,32,64,4]{2,1,3,0:T(8,128)} %get-tuple-element.168, s32[]{:T(128)} %get-tuple-element.167, bf16[64,3,8,512]{3,0,2,1:T(8,128)(2,1)S(1)} %get-tuple-element.179, f32[8,512]{1,0:T(8,128)S(1)} %broadcast_divide_fusion.2, f32[4,8,3,512]{3,1,0,2:T(8,128)S(1)} %get-tuple-element.153, ...), kind=kOutput, calls=%fused_computation.5.clone.1 | convolution fusion | flops 212336640 | bytes 3817984 | tf_op jit(solution)/shard_map/while/body/eval_jaxpr/ikedp,jdep->ijk/dot_general | solution.py:80
  113.0 3.1 %copy.24 = f32[32,64,64]{2,0,1:T(8,128)} copy(f32[32,64,64]{1,0,2:T(8,128)} %bitcast.5) | data formatting | bytes 1048576 | tf_op jit(solution)/shard_map/reshape | solution.py:85
  116.1 57.7 %reduce-scatter.2.cloned.1.call-done = f32[32,4,64]{2,0,1:T(8,128)} async-done(((f32[32,64,64]{2,0,1:T(8,128)}), f32[32,4,64]{2,0,1:T(8,128)}) %reduce-scatter.2.cloned.1.call-update) | async-done | bytes 32784 | tf_op jit(solution)/shard_map/reduce_scatter | solution.py:105
  (96 shorter events, 26.4 us)
Async XLA Ops:
  6.5 3.0 %copy-start.1 = (s32[8]{0:T(128)S(1)}, s32[8]{0:T(128)}, u32[]{:S(2)}) copy-start(s32[8]{0:T(128)} %param.8) | copy-start | bytes 100
  6.5 32.3 %all-gather.2.cloned.1.call-start = ((), (), s32[]{:S(2)}) async-start(), calls=%async_computation.1 | async-start | bytes 2359296 | tf_op jit(solution)/shard_map/all_gather | solution.py:94
  7.3 166.6 %reduce-scatter.2.cloned.1.call-start = ((), (), s32[]{:S(2)}) async-start(), calls=%async_computation.2 | async-start | bytes 1114112 | tf_op jit(solution)/shard_map/reduce_scatter | solution.py:105
  47.2 7.7 %copy-start = (f32[512]{0:T(512)S(1)}, f32[512]{0:T(512)}, u32[]{:S(2)}) copy-start(f32[512]{0:T(512)} %constant.23.clone) | copy-start | bytes 6148
Sparse Core Ops, SparseCore 0:
  8.9 29.9 all-gather.1
  116.2 57.5 reduce-scatter.1
where the time goes:
time: 183 us; the launch traced here: 182 us
  waiting for transfers between devices  87.6 us (48%)
  matrix products  41.2 us (23%)
  local copies, waits for them, and re-layouts  34.8 us (19%)
  between operations  13.5 us (7%)
  other arithmetic  4.61 us (3%)
    reduce_scatter x1, waiting for transfers between devices, body(): lax.psum_scatter(partial_value, 'elem', scatter_dimension=1, tiled=True)  57.7 us
    dot_general x16, matrix products, one_block(): jnp.einsum('ikedp,jdep->ijk', pairs, trial_fields, preferred_element_type...  34.5 us
    all_gather x1, waiting for transfers between devices, body(): gathered = lax.all_gather(mode_fields, 'test', axis=0, tiled=True)  29.2 us
    dynamic_slice x16, local copies, waits for them, and re-layouts, project(): result = lax.map(one_block, blocks)  17.1 us
    reshape x1, local copies, waits for them, and re-layouts, project(): grads.reshape((grad_modes // block_modes, block_modes) + grads.shape[1:])  7.71 us
    dot_general x1, matrix products, gradient(): jnp.dot(flat, table, preferred_element_type=jnp.float32)  6.71 us
  transfers between devices with their start and end apart: 2, of which 2 were waited for; matrix products, arithmetic and copies ran while one was open for 1% of the time, Pallas kernels for 0%

commit v1 on v0

v1 whole, which is shorter than its diff:
```python
import jax
import jax.numpy as jnp
import numpy as np
from jax import lax
from jax.experimental import pallas as pl
from jax.experimental.pallas import tpu as pltpu
from jax.sharding import PartitionSpec as P

Q = 8


block_modes = 8
rows16 = 16


def legendre_top(points, degree):
    before = points * 0.0 + 1.0
    current = points
    for order in range(2, degree + 1):
        following = ((2 * order - 1) * points * current - (order - 1) * before) / order
        before = current
        current = following
    return (current, before)


def lobatto_tables(order_points):
    degree = order_points - 1
    lobatto_nodes = np.cos(np.pi * np.arange(degree + 1) / degree)
    for sweep in range(100):
        top, lower = legendre_top(lobatto_nodes, degree)
        lobatto_nodes = lobatto_nodes - (lobatto_nodes * top - lower) / ((degree + 1) * top)
    lobatto_nodes = lobatto_nodes[::-1].copy()
    lobatto_nodes[0] = -1.0
    lobatto_nodes[-1] = 1.0
    values, unused = legendre_top(lobatto_nodes, degree)
    weights = 2.0 / (degree * (degree + 1) * values**2)
    identity = np.eye(order_points)
    distance = lobatto_nodes[:, None] - lobatto_nodes[None, :]
    spacing = np.where(identity > 0, 1.0, distance)
    derivative = np.where(identity > 0, 0.0, values[:, None] / values[None, :] / spacing)
    corner = degree * (degree + 1) / 4.0
    ends = np.concatenate([[-corner], np.zeros(degree - 1), [corner]])
    derivative = derivative + identity * ends[None, :]
    square_eye = np.eye(order_points * order_points)
    along_r = np.kron(square_eye, derivative)
    along_s = np.kron(identity, np.kron(derivative, identity))
    along_t = np.kron(derivative, square_eye)
    table = np.concatenate([along_r.T, along_s.T, along_t.T], axis=1)
    cube_weights = np.kron(weights, np.kron(weights, weights))
    return (table.astype(np.float32), cube_weights.astype(np.float32))


def kernel(
    n_test, n_elem, final_scale,
    x_ref, types, type_scales, table_rs, table_t, weights,
    out_ref,
    fields, grads, wide, rhs, totals, outgoing, incoming,
    local_sem, send_sem, recv_sem, send_sum, recv_sum,
):
    elements, _, modes, cube = x_ref.shape
    all_modes = n_test * modes
    half = cube // 2
    owned = all_modes // n_elem
    blocks = modes // block_modes
    t = lax.axis_index("test")
    me = lax.axis_index("elem")

    def local_copy(e):
        return pltpu.make_async_copy(x_ref.at[e], fields.at[t, e], local_sem.at[e])

    def panel_copy(off, e):
        return pltpu.make_async_remote_copy(
            src_ref=fields.at[t, e],
            dst_ref=fields.at[t, e],
            send_sem=send_sem.at[off - 1, e],
            recv_sem=recv_sem.at[off - 1, e],
            device_id={"test": lax.rem(t + off, n_test)},
            device_id_type=pl.DeviceIdType.MESH,
        )

    def sum_copy(off):
        return pltpu.make_async_remote_copy(
            src_ref=outgoing.at[lax.rem(me + off, n_elem)],
            dst_ref=incoming.at[off - 1],
            send_sem=send_sum.at[off - 1],
            recv_sem=recv_sum.at[off - 1],
            device_id={"elem": lax.rem(me + off, n_elem)},
            device_id_type=pl.DeviceIdType.MESH,
        )

    for e in range(elements):
        local_copy(e).start()

    barrier = pltpu.get_barrier_semaphore()
    for off in range(1, n_test):
        pl.semaphore_signal(
            barrier, inc=1, device_id={"test": lax.rem(t + off, n_test)},
            device_id_type=pl.DeviceIdType.MESH,
        )
    for off in range(1, n_elem):
        pl.semaphore_signal(
            barrier, inc=1, device_id={"elem": lax.rem(me + off, n_elem)},
            device_id_type=pl.DeviceIdType.MESH,
        )
    pl.semaphore_wait(barrier, n_test + n_elem - 2)

    for e in range(elements):
        local_copy(e).wait()
        for off in range(1, n_test):
            panel_copy(off, e).start()

    totals[...] = jnp.zeros_like(totals)

    def element(e, carry):
        for off in range(1, n_test):
            panel_copy(off, e).wait_recv()
        kind = types[e]
        scale = [type_scales[kind, d] for d in range(3)]
        volume = jnp.full((1, cube), scale[0] * scale[1] * scale[2], jnp.float32)
        quadrature = weights[...] / volume
        factor = [quadrature * scale[d] for d in range(3)]
        held = [
            jnp.concatenate([fields[n, e, c] for n in range(n_test)], axis=0) for c in range(3)
        ]
        stacked = jnp.concatenate(held, axis=0)
        for h in range(2):
            part = slice(h * half, (h + 1) * half)
            derived = jnp.dot(
                stacked[:, part], table_rs[...], preferred_element_type=jnp.float32
            )
            for d in range(2):
                grads[d, :, part] = (
                    derived[:, d * half : (d + 1) * half] * factor[d][:, part]
                ).astype(jnp.bfloat16)
        derived = jnp.dot(stacked, table_t[...], preferred_element_type=jnp.float32)
        grads[2] = (derived * factor[2]).astype(jnp.bfloat16)
        for d in range(3):
            rhs[d] = held[d].T
        for c in range(3):
            own = fields[t, e, c].astype(jnp.float32)
            for i in range(modes):
                wide[c * modes + i] = jnp.broadcast_to(own[i : i + 1], (rows16, cube)).astype(
                    jnp.bfloat16
                )

        def block(ib, inner):
            total = jnp.zeros((block_modes * all_modes, all_modes), jnp.float32)
            for d in range(3):
                for h in range(2):
                    part = slice(h * half, (h + 1) * half)
                    g = [
                        grads[d, c * all_modes : (c + 1) * all_modes, part].reshape(
                            all_modes // rows16, rows16, half
                        )
                        for c in range(3)
                    ]
                    pairs = []
                    for i in range(block_modes):
                        row = ib * block_modes + i
                        f = [wide[c * modes + row, :, part][None] for c in range(3)]
                        summed = f[0] * g[0] + f[1] * g[1] + f[2] * g[2]
                        pairs.append(summed.reshape(all_modes, half))
                    total = total + jnp.dot(
                        jnp.concatenate(pairs, axis=0),
                        rhs[d, part, :],
                        preferred_element_type=jnp.float32,
                    )
            totals[ib] += total
            return inner

        return lax.fori_loop(0, blocks, block, carry)

    lax.fori_loop(0, elements, element, 0)

    turned = [totals[ib].T for ib in range(blocks)]
    for b in range(n_elem):
        outgoing[b] = jnp.concatenate(
            [turned[ib][b * owned : (b + 1) * owned] for ib in range(blocks)], axis=0
        ).astype(jnp.bfloat16)
    for off in range(1, n_elem):
        sum_copy(off).start()
    result = outgoing[me].astype(jnp.float32)
    for off in range(1, n_elem):
        sum_copy(off).wait_recv()
        result = result + incoming[off - 1].astype(jnp.float32)
    out_ref[...] = result * final_scale

    for off in range(1, n_elem):
        sum_copy(off).wait_send()

    def drain(e, carry):
        for off in range(1, n_test):
            panel_copy(off, e).wait_send()
        return carry

    lax.fori_loop(0, elements, drain, 0)


def split_tables(order_points):
    table, cube_weights = lobatto_tables(order_points)
    cube = order_points**3
    half = cube // 2
    table_rs = np.concatenate([table[:half, :half], table[:half, cube : cube + half]], axis=1)
    table_t = table[:, 2 * cube :]
    return table_rs, table_t, cube_weights


def body(mode_fields, elem_type, type_scales):
    n_test = lax.axis_size("test")
    n_elem = lax.axis_size("elem")
    cube = Q**3
    modes, _, points = mode_fields.shape
    elements = points // cube
    all_modes = modes * n_test
    owned = all_modes // n_elem
    blocks = modes // block_modes
    table_rs, table_t, cube_weights = split_tables(Q)
    chunks = mode_fields.reshape(modes, 3, elements, cube).transpose(2, 1, 0, 3)
    final_scale = float(points * n_elem) ** (-0.5)
    rows = blocks * owned
    lanes = block_modes * all_modes
    vmem = pl.BlockSpec(memory_space=pltpu.VMEM)
    smem = pl.BlockSpec(memory_space=pltpu.SMEM)

    def call(*args):
        kernel(n_test, n_elem, final_scale, *args)

    out = pl.pallas_call(
        call,
        out_shape=jax.ShapeDtypeStruct((rows, lanes), jnp.float32),
        in_specs=[pl.BlockSpec(memory_space=pl.ANY), smem, smem, vmem, vmem, vmem],
        out_specs=vmem,
        scratch_shapes=[
            pltpu.VMEM((n_test, elements, 3, modes, cube), jnp.bfloat16),
            pltpu.VMEM((3, 3 * all_modes, cube), jnp.bfloat16),
            pltpu.VMEM((3 * modes, rows16, cube), jnp.bfloat16),
            pltpu.VMEM((3, cube, all_modes), jnp.bfloat16),
            pltpu.VMEM((blocks, lanes, all_modes), jnp.float32),
            pltpu.VMEM((n_elem, rows, lanes), jnp.bfloat16),
            pltpu.VMEM((n_elem - 1, rows, lanes), jnp.bfloat16),
            pltpu.SemaphoreType.DMA((elements,)),
            pltpu.SemaphoreType.DMA((n_test - 1, elements)),
            pltpu.SemaphoreType.DMA((n_test - 1, elements)),
            pltpu.SemaphoreType.DMA((n_elem - 1,)),
            pltpu.SemaphoreType.DMA((n_elem - 1,)),
        ],
        compiler_params=pltpu.CompilerParams(
            collective_id=0, has_side_effects=True, vmem_limit_bytes=48 * 2**20
        ),
    )(
        chunks,
        elem_type,
        type_scales,
        jnp.asarray(table_rs).astype(jnp.bfloat16),
        jnp.asarray(table_t).astype(jnp.bfloat16),
        jnp.asarray(cube_weights)[None, :],
    )
    return (
        out.reshape(blocks, owned, block_modes, all_modes)
        .transpose(0, 2, 1, 3)
        .reshape(modes, owned, all_modes)
    )


def solution(mesh):
    placed = (P("test", None, "elem"), P("elem"), P())
    return jax.shard_map(
        body, mesh=mesh, in_specs=placed, out_specs=P("test", "elem", None), check_vma=False
    )
```

time: 183 us -> 43.3 us (0.24)
  waiting for transfers between devices: 87.6 us -> 0 us
  matrix products: 41.2 us -> 0 us
  Pallas kernels: 0 us -> 40.4 us
  local copies, waits for them, and re-layouts: 34.8 us -> 2.68 us
  between operations: 13.5 us -> 0.06 us
  other arithmetic: 4.61 us -> 0 us
    reduce_scatter x1 -> x0, waiting for transfers between devices: 57.7 us -> none  [body(): lax.psum_scatter(partial_value, 'elem', scatter_dimension=1, tiled=True)]
    dot_general x17 -> x0, matrix products: 41.2 us -> none  [the longest x16 34.5 us: one_block(): jnp.einsum('ikedp,jdep->ijk', pairs, trial_fields, preferred_element_type...]
    pallas_call x0 -> x1, Pallas kernels: none -> 40.4 us  [body(): pl.pallas_call(call, out_shape=jax.ShapeDtypeStruct((rows, lanes), jnp.fl...]
    all_gather x1 -> x0, waiting for transfers between devices: 29.2 us -> none  [body(): gathered = lax.all_gather(mode_fields, 'test', axis=0, tiled=True)]
    dynamic_slice x16 -> x0, local copies, waits for them, and re-layouts: 17.1 us -> none  [project(): result = lax.map(one_block, blocks)]
    reshape x2, local copies, waits for them, and re-layouts: 10.8 us -> 1.37 us  [the longest x1 1.29 us: body(): chunks = mode_fields.reshape(modes, 3, elements, cube).transpose(2, 1, 0, 3)]
    mul x33 -> x0, local copies, waits for them, and re-layouts: 4.29 us -> none  [the longest x32 3.61 us: one_block(): summed = test_wide[:, None, 0, :, None, :] * grad_wide[None, :, 0]]
    convert_element_type x18 -> x0, other arithmetic: 2.48 us -> none  [the longest x1 1.26 us: project(): test_wide = test_fields.astype(jnp.float32)]
  transfers between devices with their start and end apart: 2 -> 0, of which waited for: 2 -> 0; matrix products, arithmetic and copies ran while one was open for 1% -> 0% of each run, Pallas kernels for 0% -> 0%
where the time goes in v1:
time: 43.3 us; the launch traced here: 43.2 us
  Pallas kernels  40.4 us (93%)
  local copies, waits for them, and re-layouts  2.68 us (6%)
    pallas_call x1, Pallas kernels, body(): pl.pallas_call(call, out_shape=jax.ShapeDtypeStruct((rows, lanes), jnp.fl...  40.4 us
    reshape x1, local copies, waits for them, and re-layouts, body(): chunks = mode_fields.reshape(modes, 3, elements, cube).transpose(2, 1, 0, 3)  1.29 us

profile of v1, /device:TPU:0, one launch (start us, length us, event | category | flops | bytes accessed | tf_op | source)
XLA Modules:
  0.0 43.2 jit_solution(13156641519307873613)
XLA Ops:
  0.0 0.0 copy-start
  0.0 0.0 copy-start.1
  0.0 0.0 copy-start.3
  0.0 1.3 %copy.12 = bf16[3,4,8,8,512]{4,3,1,0,2:T(8,128)(2,1)S(1)} copy(bf16[3,4,8,8,512]{4,3,2,1,0:T(8,128)(2,1)} %bitcast.10) | data formatting | bytes 1572864 | tf_op jit(solution)/shard_map/reshape | solution.py:218
  1.3 0.0 copy-start.2
  1.3 0.0 copy-start.4
  1.3 0.0 copy-done
  1.3 0.0 copy-done.1
  1.3 0.0 copy-done.3
  1.4 0.6 %copy-done.2 = f32[4,3]{1,0:T(4,128)S(1)} copy-done((f32[4,3]{1,0:T(4,128)S(1)}, f32[4,3]{1,0:T(4,128)}, u32[]{:S(2)}) %copy-start.2) | copy-done | bytes 72
  2.0 0.0 copy-done.4
  2.0 40.4 %shard_map.64 = f32[16,512]{1,0:T(8,128)S(1)} custom-call(bf16[8,3,32,512]{3,2,1,0:T(8,128)(2,1)S(1)} %bitcast.9, s32[8]{0:T(128)S(1)} %copy-done.4, f32[4,3]{1,0:T(4,128)S(1)} %copy-done.2, bf16[256,512]{1,0:T(8,128)(2,1)S(1)} %copy-done.1, bf16[512,512]{1,0:T(8,128)(2,1)S(1)} %copy-done, f32[1,512]{1,0:T(1,128)S(1)} %copy-done.3), custom_call_target="tpu_custom_call" | custom-call | tf_op jit(solution)/shard_map/pallas_call | solution.py:228
  42.4 0.1 reshape.10
  42.5 0.6 %copy.9 = f32[4,8,4,64]{3,2,1,0:T(4,128)} copy(f32[4,8,4,64]{3,1,2,0:T(8,128)S(1)} %bitcast.11) | data formatting | bytes 65536 | tf_op jit(solution)/shard_map/transpose | solution.py:260
Async XLA Ops:
  0.0 1.3 %copy-start = (bf16[512,512]{1,0:T(8,128)(2,1)S(1)}, bf16[512,512]{1,0:T(8,128)(2,1)}, u32[]{:S(2)}) copy-start(bf16[512,512]{1,0:T(8,128)(2,1)} %constant.11.args_4_) | copy-start | bytes 1572868
  0.0 1.3 %copy-start.1 = (bf16[256,512]{1,0:T(8,128)(2,1)S(1)}, bf16[256,512]{1,0:T(8,128)(2,1)}, u32[]{:S(2)}) copy-start(bf16[256,512]{1,0:T(8,128)(2,1)} %constant.10.args_3_) | copy-start | bytes 786436
  0.0 1.3 %copy-start.3 = (f32[1,512]{1,0:T(1,128)S(1)}, f32[1,512]{1,0:T(1,128)}, u32[]{:S(2)}) copy-start(f32[1,512]{1,0:T(1,128)} %constant.12.args_5_) | copy-start | bytes 6148
  1.3 0.7 %copy-start.2 = (f32[4,3]{1,0:T(4,128)S(1)}, f32[4,3]{1,0:T(4,128)}, u32[]{:S(2)}) copy-start(f32[4,3]{1,0:T(4,128)} %args_2_.4) | copy-start | bytes 148
  1.3 0.7 %copy-start.4 = (s32[8]{0:T(128)S(1)}, s32[8]{0:T(128)}, u32[]{:S(2)}) copy-start(s32[8]{0:T(128)} %args_1_.4) | copy-start | bytes 100

commit v2 on v1

v2 whole, which is shorter than its diff:
```python
import jax
import jax.numpy as jnp
import numpy as np
from jax import lax
from jax.experimental import pallas as pl
from jax.experimental.pallas import tpu as pltpu
from jax.sharding import PartitionSpec as P

Q = 8


block_modes = 8
rows16 = 16
lane_width = 128
tail_elements = 2


def legendre_top(points, degree):
    before = points * 0.0 + 1.0
    current = points
    for order in range(2, degree + 1):
        following = ((2 * order - 1) * points * current - (order - 1) * before) / order
        before = current
        current = following
    return (current, before)


def lobatto_tables(order_points):
    degree = order_points - 1
    lobatto_nodes = np.cos(np.pi * np.arange(degree + 1) / degree)
    for sweep in range(100):
        top, lower = legendre_top(lobatto_nodes, degree)
        lobatto_nodes = lobatto_nodes - (lobatto_nodes * top - lower) / ((degree + 1) * top)
    lobatto_nodes = lobatto_nodes[::-1].copy()
    lobatto_nodes[0] = -1.0
    lobatto_nodes[-1] = 1.0
    values, unused = legendre_top(lobatto_nodes, degree)
    weights = 2.0 / (degree * (degree + 1) * values**2)
    identity = np.eye(order_points)
    distance = lobatto_nodes[:, None] - lobatto_nodes[None, :]
    spacing = np.where(identity > 0, 1.0, distance)
    derivative = np.where(identity > 0, 0.0, values[:, None] / values[None, :] / spacing)
    corner = degree * (degree + 1) / 4.0
    ends = np.concatenate([[-corner], np.zeros(degree - 1), [corner]])
    derivative = derivative + identity * ends[None, :]
    square_eye = np.eye(order_points * order_points)
    along_r = np.kron(square_eye, derivative)
    along_s = np.kron(identity, np.kron(derivative, identity))
    along_t = np.kron(derivative, square_eye)
    table = np.concatenate([along_r.T, along_s.T, along_t.T], axis=1)
    cube_weights = np.kron(weights, np.kron(weights, weights))
    return (table.astype(np.float32), cube_weights.astype(np.float32))


def kernel(
    n_test, n_elem, elements, final_scale,
    x_ref, types, type_scales, far_rs, far_t, weights,
    out_ref,
    table_rs, table_t, table_sem, fields, grads, wide, rhs, totals, outgoing, incoming,
    local_sem, send_sem, recv_sem, send_sum, recv_sum,
):
    _, modes, points = x_ref.shape
    cube = points // elements
    all_modes = n_test * modes
    half = cube // 2
    owned = all_modes // n_elem
    blocks = modes // block_modes
    parts = block_modes * all_modes // lane_width
    tail = min(tail_elements, elements)
    t = lax.axis_index("test")
    me = lax.axis_index("elem")

    def local_copy(e):
        return pltpu.make_async_copy(
            x_ref.at[:, :, pl.ds(e * cube, cube)], fields.at[t, e], local_sem.at[e]
        )

    def panel_copy(off, e):
        return pltpu.make_async_remote_copy(
            src_ref=fields.at[t, e],
            dst_ref=fields.at[t, e],
            send_sem=send_sem.at[off - 1, e],
            recv_sem=recv_sem.at[off - 1, e],
            device_id={"test": lax.rem(t + off, n_test)},
            device_id_type=pl.DeviceIdType.MESH,
        )

    def sum_copy(off, ib):
        return pltpu.make_async_remote_copy(
            src_ref=outgoing.at[ib, lax.rem(me + off, n_elem)],
            dst_ref=incoming.at[ib, off - 1],
            send_sem=send_sum.at[ib, off - 1],
            recv_sem=recv_sum.at[ib, off - 1],
            device_id={"elem": lax.rem(me + off, n_elem)},
            device_id_type=pl.DeviceIdType.MESH,
        )

    barrier = pltpu.get_barrier_semaphore()
    for off in range(1, n_test):
        pl.semaphore_signal(
            barrier, inc=1, device_id={"test": lax.rem(t + off, n_test)},
            device_id_type=pl.DeviceIdType.MESH,
        )
    for off in range(1, n_elem):
        pl.semaphore_signal(
            barrier, inc=1, device_id={"elem": lax.rem(me + off, n_elem)},
            device_id_type=pl.DeviceIdType.MESH,
        )
    for e in range(elements):
        local_copy(e).start()
    tables = [
        pltpu.make_async_copy(far_rs, table_rs, table_sem.at[0]),
        pltpu.make_async_copy(far_t, table_t, table_sem.at[1]),
    ]
    for copy in tables:
        copy.start()
    pl.semaphore_wait(barrier, n_test + n_elem - 2)

    for e in range(elements):
        local_copy(e).wait()
        for off in range(1, n_test):
            panel_copy(off, e).start()

    for copy in tables:
        copy.wait()

    def differentiate(n, e):
        kind = types[e]
        scale = [type_scales[kind, d] for d in range(3)]
        volume = jnp.full((1, cube), scale[0] * scale[1] * scale[2], jnp.float32)
        quadrature = weights[...] / volume
        factor = [quadrature * scale[d] for d in range(3)]
        stacked = jnp.concatenate([fields[n, e, c] for c in range(3)], axis=0)
        for h in range(2):
            part = slice(h * half, (h + 1) * half)
            derived = jnp.dot(
                stacked[:, part], table_rs[...], preferred_element_type=jnp.float32
            )
            for d in range(2):
                value = derived[:, d * half : (d + 1) * half] * factor[d][:, part]
                for c in range(3):
                    grads[e, d, c, n, :, part] = value[c * modes : (c + 1) * modes].astype(
                        jnp.bfloat16
                    )
        value = jnp.dot(stacked, table_t[...], preferred_element_type=jnp.float32) * factor[2]
        for c in range(3):
            grads[e, 2, c, n] = value[c * modes : (c + 1) * modes].astype(jnp.bfloat16)

    def own_panel(e, carry):
        differentiate(t, e)
        for c in range(3):
            own = fields[t, e, c].astype(jnp.float32)
            for i in range(modes):
                wide[e, c * modes + i] = jnp.broadcast_to(
                    own[i : i + 1], (rows16, cube)
                ).astype(jnp.bfloat16)
        return carry

    lax.fori_loop(0, elements, own_panel, 0)
    totals[...] = jnp.zeros_like(totals)

    def arrive(e):
        for off in range(1, n_test):
            panel_copy(off, e).wait_recv()
            differentiate(lax.rem(t + n_test - off, n_test), e)
        for d in range(3):
            rhs[e, d] = jnp.concatenate([fields[n, e, d] for n in range(n_test)], axis=0).T

    def block(e, ib):
        total = jnp.zeros((block_modes * all_modes, all_modes), jnp.float32)
        for d in range(3):
            for h in range(2):
                part = slice(h * half, (h + 1) * half)
                g = [
                    grads[e, d, c, :, :, part].reshape(all_modes // rows16, rows16, half)
                    for c in range(3)
                ]
                pairs = []
                for i in range(block_modes):
                    row = ib * block_modes + i
                    f = [wide[e, c * modes + row, :, part][None] for c in range(3)]
                    summed = f[0] * g[0] + f[1] * g[1] + f[2] * g[2]
                    pairs.append(summed.reshape(all_modes, half))
                total = total + jnp.dot(
                    jnp.concatenate(pairs, axis=0),
                    rhs[e, d, part, :],
                    preferred_element_type=jnp.float32,
                )
        totals[ib] += total

    def loop(start, stop, work):
        def step(index, carry):
            work(index)
            return carry

        lax.fori_loop(start, stop, step, 0)

    def element(e):
        arrive(e)
        loop(0, blocks, lambda ib: block(e, ib))

    loop(0, elements - tail, element)
    loop(elements - tail, elements, arrive)

    def finish(ib):
        loop(elements - tail, elements, lambda e: block(e, ib))
        turned = totals[ib].T
        for b in range(n_elem):
            rows = turned[b * owned : (b + 1) * owned]
            outgoing[ib, b] = jnp.concatenate(
                [rows[:, q * lane_width : (q + 1) * lane_width] for q in range(parts)], axis=0
            ).astype(jnp.bfloat16)
        for off in range(1, n_elem):
            sum_copy(off, ib).start()

    loop(0, blocks, finish)

    def drain(e):
        for off in range(1, n_test):
            panel_copy(off, e).wait_send()

    loop(0, elements, drain)

    def collect(ib):
        result = outgoing[ib, me].astype(jnp.float32)
        for off in range(1, n_elem):
            sum_copy(off, ib).wait_recv()
            result = result + incoming[ib, off - 1].astype(jnp.float32)
        out_ref[ib] = result * final_scale
        for off in range(1, n_elem):
            sum_copy(off, ib).wait_send()

    loop(0, blocks, collect)


def split_tables(order_points):
    table, cube_weights = lobatto_tables(order_points)
    cube = order_points**3
    half = cube // 2
    table_rs = np.concatenate([table[:half, :half], table[:half, cube : cube + half]], axis=1)
    table_t = table[:, 2 * cube :]
    return table_rs, table_t, cube_weights


def body(mode_fields, elem_type, type_scales):
    n_test = lax.axis_size("test")
    n_elem = lax.axis_size("elem")
    cube = Q**3
    modes, _, points = mode_fields.shape
    elements = points // cube
    all_modes = modes * n_test
    owned = all_modes // n_elem
    blocks = modes // block_modes
    table_rs, table_t, cube_weights = split_tables(Q)
    final_scale = float(points * n_elem) ** (-0.5)
    lanes = block_modes * all_modes
    parts = lanes // lane_width
    rows = parts * owned
    vmem = pl.BlockSpec(memory_space=pltpu.VMEM)
    far = pl.BlockSpec(memory_space=pl.ANY)
    smem = pl.BlockSpec(memory_space=pltpu.SMEM)

    def call(*args):
        kernel(n_test, n_elem, elements, final_scale, *args)

    out = pl.pallas_call(
        call,
        out_shape=jax.ShapeDtypeStruct((blocks, rows, lane_width), jnp.float32),
        in_specs=[far, smem, smem, far, far, vmem],
        out_specs=vmem,
        scratch_shapes=[
            pltpu.VMEM(table_rs.shape, jnp.bfloat16),
            pltpu.VMEM(table_t.shape, jnp.bfloat16),
            pltpu.SemaphoreType.DMA((2,)),
            pltpu.VMEM((n_test, elements, 3, modes, cube), jnp.bfloat16),
            pltpu.VMEM((elements, 3, 3, n_test, modes, cube), jnp.bfloat16),
            pltpu.VMEM((elements, 3 * modes, rows16, cube), jnp.bfloat16),
            pltpu.VMEM((elements, 3, cube, all_modes), jnp.bfloat16),
            pltpu.VMEM((blocks, lanes, all_modes), jnp.float32),
            pltpu.VMEM((blocks, n_elem, rows, lane_width), jnp.bfloat16),
            pltpu.VMEM((blocks, n_elem - 1, rows, lane_width), jnp.bfloat16),
            pltpu.SemaphoreType.DMA((elements,)),
            pltpu.SemaphoreType.DMA((n_test - 1, elements)),
            pltpu.SemaphoreType.DMA((n_test - 1, elements)),
            pltpu.SemaphoreType.DMA((blocks, n_elem - 1)),
            pltpu.SemaphoreType.DMA((blocks, n_elem - 1)),
        ],
        compiler_params=pltpu.CompilerParams(
            collective_id=0, has_side_effects=True, vmem_limit_bytes=60 * 1024 * 2**10
        ),
    )(
        mode_fields.transpose(1, 0, 2),
        elem_type,
        type_scales,
        jnp.asarray(table_rs).astype(jnp.bfloat16),
        jnp.asarray(table_t).astype(jnp.bfloat16),
        jnp.asarray(cube_weights)[None, :],
    )
    return (
        out.reshape(blocks, parts, owned, lane_width // all_modes, all_modes)
        .transpose(0, 1, 3, 2, 4)
        .reshape(modes, owned, all_modes)
    )


def solution(mesh):
    placed = (P("test", None, "elem"), P("elem"), P())
    return jax.shard_map(
        body, mesh=mesh, in_specs=placed, out_specs=P("test", "elem", None), check_vma=False
    )
```

time: 43.3 us -> 40.4 us (0.933)
  Pallas kernels: 40.4 us -> 38.7 us
  local copies, waits for them, and re-layouts: 2.68 us -> 1.5 us
    pallas_call x1, Pallas kernels: 40.4 us -> 38.7 us  [body(): pl.pallas_call(call, out_shape=jax.ShapeDtypeStruct((blocks, rows, lane_w...]
    unnamed x10 -> x0, local copies, waits for them, and re-layouts: 0.67 us -> none
    reshape x2 -> x1, local copies, waits for them, and re-layouts: 1.37 us -> 0.85 us  [body(): out.reshape(blocks, parts, owned, lane_width // all_modes, all_modes)]
where the time goes in v2:
time: 40.4 us; the launch traced here: 40.2 us
  Pallas kernels  38.7 us (96%)
  local copies, waits for them, and re-layouts  1.5 us (4%)
    pallas_call x1, Pallas kernels, body(): pl.pallas_call(call, out_shape=jax.ShapeDtypeStruct((blocks, rows, lane_w...  38.7 us
    reshape x1, local copies, waits for them, and re-layouts, body(): out.reshape(blocks, parts, owned, lane_width // all_modes, all_modes)  0.85 us

profile of v2, /device:TPU:0, one launch (start us, length us, event | category | flops | bytes accessed | tf_op | source)
XLA Modules:
  0.0 40.2 jit_solution(2018754099654635197)
XLA Ops:
  0.0 38.7 %shard_map.64 = f32[4,16,128]{2,1,0:T(8,128)} custom-call(bf16[3,32,4096]{2,1,0:T(8,128)(2,1)} %bitcast.3, s32[8]{0:T(128)} %args_1_.4, f32[4,3]{1,0:T(4,128)} %args_2_.4, bf16[256,512]{1,0:T(8,128)(2,1)} %constant.10.args_3_, bf16[512,512]{1,0:T(8,128)(2,1)} %constant.11.args_4_, f32[1,512]{1,0:T(1,128)} %constant.12.args_5_), custom_call_target="tpu_custom_call" | custom-call | tf_op jit(solution)/shard_map/pallas_call | solution.py:266
  38.7 0.9 %reshape.6 = f32[4,4,4,2,64]{4,3,2,1,0:T(2,128)S(1)} reshape(f32[4,16,128]{2,1,0:T(8,128)} %shard_map.64) | data formatting | bytes 65536 | tf_op jit(solution)/shard_map/reshape | solution.py:300
  39.6 0.6 %copy.7 = f32[4,4,2,4,64]{4,3,2,1,0:T(4,128)} copy(f32[4,4,2,4,64]{4,2,3,1,0:T(2,128)S(1)} %bitcast.4) | data formatting | bytes 65536 | tf_op jit(solution)/shard_map/transpose | solution.py:301

commit v3 on v2

--- a/solution.py
+++ b/solution.py
@@ -10,6 +10,7 @@
 
 
 block_modes = 8
+many_modes = 16
 rows16 = 16
 lane_width = 128
 tail_elements = 2
@@ -67,6 +68,7 @@
     blocks = modes // block_modes
     parts = block_modes * all_modes // lane_width
     tail = min(tail_elements, elements)
+    many = many_modes if modes % many_modes == 0 else block_modes
     t = lax.axis_index("test")
     me = lax.axis_index("elem")
 
@@ -166,8 +168,8 @@
         for d in range(3):
             rhs[e, d] = jnp.concatenate([fields[n, e, d] for n in range(n_test)], axis=0).T
 
-    def block(e, ib):
-        total = jnp.zeros((block_modes * all_modes, all_modes), jnp.float32)
+    def block(e, step, count):
+        total = jnp.zeros((count * all_modes, all_modes), jnp.float32)
         for d in range(3):
             for h in range(2):
                 part = slice(h * half, (h + 1) * half)
@@ -176,8 +178,8 @@
                     for c in range(3)
                 ]
                 pairs = []
-                for i in range(block_modes):
-                    row = ib * block_modes + i
+                for i in range(count):
+                    row = step * count + i
                     f = [wide[e, c * modes + row, :, part][None] for c in range(3)]
                     summed = f[0] * g[0] + f[1] * g[1] + f[2] * g[2]
                     pairs.append(summed.reshape(all_modes, half))
@@ -186,7 +188,10 @@
                     rhs[e, d, part, :],
                     preferred_element_type=jnp.float32,
                 )
-        totals[ib] += total
+        held = count // block_modes
+        lanes = block_modes * all_modes
+        for b in range(held):
+            totals[step * held + b] += total[b * lanes : (b + 1) * lanes]
 
     def loop(start, stop, work):
         def step(index, carry):
@@ -197,13 +202,13 @@
 
     def element(e):
         arrive(e)
-        loop(0, blocks, lambda ib: block(e, ib))
+        loop(0, modes // many, lambda step: block(e, step, many))
 
     loop(0, elements - tail, element)
     loop(elements - tail, elements, arrive)
 
     def finish(ib):
-        loop(elements - tail, elements, lambda e: block(e, ib))
+        loop(elements - tail, elements, lambda e: block(e, ib, block_modes))
         turned = totals[ib].T
         for b in range(n_elem):
             rows = turned[b * owned : (b + 1) * owned]

time: 40.4 us -> 38.2 us (0.946)
  Pallas kernels: 38.7 us -> 36.5 us
    pallas_call x1, Pallas kernels: 38.7 us -> 36.5 us  [body(): pl.pallas_call(call, out_shape=jax.ShapeDtypeStruct((blocks, rows, lane_w...]
where the time goes in v3:
time: 38.2 us; the launch traced here: 38 us
  Pallas kernels  36.5 us (96%)
  local copies, waits for them, and re-layouts  1.5 us (4%)
    pallas_call x1, Pallas kernels, body(): pl.pallas_call(call, out_shape=jax.ShapeDtypeStruct((blocks, rows, lane_w...  36.5 us
    reshape x1, local copies, waits for them, and re-layouts, body(): out.reshape(blocks, parts, owned, lane_width // all_modes, all_modes)  0.85 us

profile of v3, /device:TPU:0, one launch (start us, length us, event | category | flops | bytes accessed | tf_op | source)
XLA Modules:
  0.0 38.0 jit_solution(15296453843491264529)
XLA Ops:
  0.0 36.5 %shard_map.64 = f32[4,16,128]{2,1,0:T(8,128)} custom-call(bf16[3,32,4096]{2,1,0:T(8,128)(2,1)} %bitcast.3, s32[8]{0:T(128)} %args_1_.4, f32[4,3]{1,0:T(4,128)} %args_2_.4, bf16[256,512]{1,0:T(8,128)(2,1)} %constant.10.args_3_, bf16[512,512]{1,0:T(8,128)(2,1)} %constant.11.args_4_, f32[1,512]{1,0:T(1,128)} %constant.12.args_5_), custom_call_target="tpu_custom_call" | custom-call | tf_op jit(solution)/shard_map/pallas_call | solution.py:271
  36.5 0.9 %reshape.6 = f32[4,4,4,2,64]{4,3,2,1,0:T(2,128)S(1)} reshape(f32[4,16,128]{2,1,0:T(8,128)} %shard_map.64) | data formatting | bytes 65536 | tf_op jit(solution)/shard_map/reshape | solution.py:305
  37.4 0.6 %copy.7 = f32[4,4,2,4,64]{4,3,2,1,0:T(4,128)} copy(f32[4,4,2,4,64]{4,2,3,1,0:T(2,128)S(1)} %bitcast.4) | data formatting | bytes 65536 | tf_op jit(solution)/shard_map/transpose | solution.py:306
